TPU v7x, 32 devices: a whole 2x2x4 slice. The times are simulated.
32 devices in a mesh: wide: 16 (over z, y, x), narrow: 2 (over core).
Axes of the slice: x: 2, y: 2, z: 4, core: 2. Of those that a mesh axis runs over, the one named last changes fastest.
Arguments:
- tokens: bfloat16 [2048, 2048], P('wide'), may hold values from -6 to 6
- expert_ids: int32 [2048, 6], P('wide'), may hold values from 0 to 15, all different within a row; in each aligned block of 128 rows (0 to 127, 128 to 255, ...) at most 64 rows name the same one
- gate_weights: float32 [2048, 6], P('wide'), may hold values from 0.05 to 0.6
- shared_gate: bfloat16 [2048, 2816], P('wide', 'narrow'), may hold values from -0.125 to 0.125
- shared_up: bfloat16 [2048, 2816], P('wide', 'narrow'), may hold values from -0.125 to 0.125
- shared_down: bfloat16 [2816, 2048], P('narrow', 'wide'), may hold values from -0.109375 to 0.109375
- expert_gate: bfloat16 [16, 2048, 1408], P('wide', None, 'narrow'), may hold values from -0.125 to 0.125
- expert_up: bfloat16 [16, 2048, 1408], P('wide', None, 'narrow'), may hold values from -0.125 to 0.125
- expert_down: bfloat16 [16, 1408, 2048], P('wide', 'narrow'), may hold values from -0.15625 to 0.15625
Outputs:
- moe_out: bfloat16 [2048, 2048], P('wide', 'narrow')
Inputs may be any that keep to these rules, and one draw needn't show every extreme that they name: `expert_ids`: the 6 ids of a row differ. Among the 128 rows of one index of wide, no expert is named by more than 64 rows.
All inputs are finite; a program needn't handle non-finite values.
Results may differ from a plain program's by a relative error of at most 0.0075.
Values may be sent and summed in bfloat16 or wider, within the bound.
A program may use at most 128 MiB of HBM per device.

v0:
```python
import jax
import jax.numpy as jnp
from jax import lax
from jax.sharding import PartitionSpec as P


def expert_ffn(received, w_gate, w_up, w_down):
    senders, items, width = received.shape
    flat_rows = received.reshape(senders * items, width)
    gate_part = jnp.dot(flat_rows, w_gate, preferred_element_type=jnp.float32)
    up_part = jnp.dot(flat_rows, w_up, preferred_element_type=jnp.float32)
    hidden = (jax.nn.silu(gate_part) * up_part).astype(jnp.bfloat16)
    partial_value = jnp.dot(hidden, w_down, preferred_element_type=jnp.float32).astype(jnp.bfloat16)
    return partial_value.reshape(senders, items, w_down.shape[1])


def body(
    tokens,
    expert_ids,
    gate_weights,
    shared_gate,
    shared_up,
    shared_down,
    expert_gate,
    expert_up,
    expert_down,
):
    tok_count, width = tokens.shape
    top_count = expert_ids.shape[1]
    experts = lax.axis_size("wide") * expert_gate.shape[0]
    capacity = min(tok_count, 4 * tok_count * top_count // (3 * experts))
    narrow_count = lax.axis_size("narrow")
    w_gate = expert_gate[0]
    w_up = expert_up[0]
    w_down = expert_down[0]
    pairs = tok_count * top_count
    flat_ids = expert_ids.reshape(pairs)
    onehot = (flat_ids[:, None] == jnp.arange(experts, dtype=jnp.int32)[None, :]).astype(jnp.int32)
    before = jnp.cumsum(onehot, axis=0) - onehot
    slot_pos = jnp.sum(before * onehot, axis=1)
    target_slot = flat_ids * capacity + slot_pos
    source = (
        jnp.full((experts * capacity,), -1, jnp.int32)
        .at[target_slot]
        .set(jnp.arange(pairs, dtype=jnp.int32))
    )
    filled = source >= 0
    token_of = jnp.where(filled, source // top_count, 0)
    outgoing = jnp.where(filled[:, None], tokens[token_of], jnp.zeros((), jnp.bfloat16))
    outgoing = outgoing.reshape(experts, capacity, width)
    quarter = capacity // narrow_count
    own_rows = lax.dynamic_slice_in_dim(outgoing, lax.axis_index("narrow") * quarter, quarter, 1)
    arrived = lax.all_to_all(own_rows, "wide", split_axis=0, concat_axis=0, tiled=True)
    joined = lax.all_gather(arrived, "narrow", axis=1, tiled=True)
    partial_value = expert_ffn(joined, w_gate, w_up, w_down)
    expert_out = (
        lax.psum_scatter(partial_value, "narrow", scatter_dimension=2, tiled=True)
        .astype(jnp.float32)
        .astype(jnp.bfloat16)
    )
    returned = lax.all_to_all(expert_out, "wide", split_axis=0, concat_axis=0, tiled=True)
    returned_rows = returned.reshape(experts * capacity, returned.shape[2])
    pair_rows = returned_rows[target_slot].astype(jnp.float32)
    weighted = gate_weights.reshape(pairs, 1) * pair_rows
    routed = jnp.sum(weighted.reshape(tok_count, top_count, returned.shape[2]), axis=1)
    gate_sum = jnp.dot(
        tokens,
        lax.all_gather(shared_gate, "wide", axis=0, tiled=True),
        preferred_element_type=jnp.float32,
    )
    up_sum = jnp.dot(
        tokens,
        lax.all_gather(shared_up, "wide", axis=0, tiled=True),
        preferred_element_type=jnp.float32,
    )
    shared_hidden = (jax.nn.silu(gate_sum) * up_sum).astype(jnp.bfloat16)
    shared_terms = jnp.dot(
        shared_hidden,
        lax.all_gather(shared_down, "wide", axis=1, tiled=True),
        preferred_element_type=jnp.float32,
    )
    shared = lax.psum_scatter(shared_terms, "narrow", scatter_dimension=1, tiled=True)
    return (shared + routed).astype(jnp.bfloat16)


def solution(mesh):
    in_specs = (
        P("wide", None),
        P("wide", None),
        P("wide", None),
        P("wide", "narrow"),
        P("wide", "narrow"),
        P("narrow", "wide"),
        P("wide", None, "narrow"),
        P("wide", None, "narrow"),
        P("wide", "narrow", None),
    )
    out_specs = P("wide", "narrow")
    return jax.shard_map(body, mesh=mesh, in_specs=in_specs, out_specs=out_specs, check_vma=False)
```

profile of v0, /device:TPU:0, one launch (start us, length us, event | category | flops | bytes accessed | tf_op | source)
XLA Modules:
  0.0 462.6 jit_solution(8130816217768334769)
XLA Ops:
  7.4 0.8 broadcast_multiply_fusion
  8.2 0.9 copy.13
  9.1 0.1 eq.29
  9.3 0.1 eq.25
  9.4 0.1 copy.12
  9.5 0.1 mul.50
  9.7 1.7 reduce-window.6
  11.4 0.3 slice_reduce_fusion
  11.7 0.1 fusion.14
  11.8 3.4 scatter_custom_fusion
  15.4 6.0 %gather_fusion = bf16[1024,2048]{1,0:T(8,128)(2,1)} fusion(bf16[128,2048]{1,0:T(8,128)(2,1)S(1)} %copy-done.1, s32[1024]{0:T(1024)S(1)} %fusion.17), kind=kCustom, calls=%fused_computation | custom fusion | bytes 8392704 | tf_op jit(solution)/shard_map/gather | solution.py:49
  21.4 2.0 dynamic-slice_select_fusion
  23.4 57.0 %all_to_all.10 = bf16[16,32,2048]{2,1,0:T(8,128)(2,1)} all-to-all(bf16[16,32,2048]{2,1,0:T(8,128)(2,1)S(1)} %dynamic-slice_select_fusion), channel_id=1, replica_groups=mesh['wide'=16,'narrow'=2] {'wide'}, dimensions={0} | all-to-all | bytes 4194304 | tf_op jit(solution)/shard_map/all_to_all | solution.py:53
  80.5 12.1 %all-gather.11.cloned.1.call-done = bf16[16,64,2048]{2,1,0:T(8,128)(2,1)} async-done(((bf16[16,32,2048]{2,1,0:T(8,128)(2,1)}), bf16[16,64,2048]{2,1,0:T(8,128)(2,1)}) %all-gather.11.cloned.1.call-update) | async-done | bytes 4194320 | tf_op jit(solution)/shard_map/all_gather | solution.py:54
  92.6 7.9 %fusion.1 = f32[1024,704]{0,1:T(8,128)} fusion(bf16[1024,2048]{1,0:T(8,128)(2,1)} %bitcast.48, bf16[1,2048,704]{1,2,0:T(8,128)(2,1)} %param.16), kind=kOutput, calls=%fused_computation.6 | convolution fusion | flops 2952790016 | bytes 9961472 | tf_op jit(solution)/shard_map/dot_general | solution.py:11
  100.5 11.3 %convolution_convert_fusion = bf16[1024,2048]{1,0:T(8,128)(2,1)} fusion(bf16[1,704,2048]{2,1,0:T(8,128)(2,1)S(1)} %copy-done, f32[1024,704]{0,1:T(8,128)} %fusion.1, bf16[1024,2048]{1,0:T(8,128)(2,1)} %bitcast.49, bf16[1,2048,704]{1,2,0:T(8,128)(2,1)} %param.15), kind=kOutput, calls=%fused_computation.4 | convolution fusion | flops 5912002560 | bytes 17039360 | tf_op jit(solution)/shard_map/dot_general | solution.py:13
  111.9 0.5 all-gather.5.cloned.1.call-update
  112.4 0.5 all-gather.7.cloned.1.call-update
  113.0 0.5 all-gather.9.cloned.1.call-update
  113.6 11.5 %reduce-scatter.5.cloned.1.call-done = bf16[16,64,1024]{2,1,0:T(8,128)(2,1)} async-done(((bf16[16,64,2048]{2,1,0:T(8,128)(2,1)}), bf16[16,64,1024]{2,1,0:T(8,128)(2,1)}) %reduce-scatter.5.cloned.1.call-update) | async-done | bytes 2097168 | tf_op jit(solution)/shard_map/reduce_scatter | solution.py:57
  125.0 7.0 %all-to-all-start.1 = ((bf16[16,64,1024]{2,1,0:T(8,128)(2,1)}), bf16[16,64,1024]{2,1,0:T(8,128)(2,1)}, u32[]{:S(2)}, u32[]{:S(2)}) async-start(bf16[16,64,1024]{2,1,0:T(8,128)(2,1)} %reduce-scatter.5.cloned.1.call-done), calls=%async_computation.3 | async-start | bytes 4194304 | tf_op jit(solution)/shard_map/all_to_all | solution.py:61
  132.0 0.2 reduce-scatter.3.cloned.1.call-start
  132.2 100.1 %all-gather.5.cloned.1.call-done = bf16[2048,1408]{1,0:T(8,128)(2,1)} async-done(((bf16[128,1408]{1,0:T(8,128)(2,1)}), bf16[2048,1408]{1,0:T(8,128)(2,1)}) %all-gather.5.cloned.1.call-update) | async-done | bytes 5767184 | tf_op jit(solution)/shard_map/all_gather | solution.py:68
  232.3 4.5 fusion.24
  236.8 85.5 %all-gather.7.cloned.1.call-done = bf16[2048,1408]{1,0:T(8,128)(2,1)} async-done(((bf16[128,1408]{1,0:T(8,128)(2,1)}), bf16[2048,1408]{1,0:T(8,128)(2,1)}) %all-gather.7.cloned.1.call-update) | async-done | bytes 5767184 | tf_op jit(solution)/shard_map/all_gather | solution.py:73
  322.4 109.5 %all-gather.9.cloned.1.call-done = bf16[1408,2048]{1,0:T(8,128)(2,1)} async-done(((bf16[1408,128]{1,0:T(8,128)(2,1)}), bf16[1408,2048]{1,0:T(8,128)(2,1)}) %all-gather.9.cloned.1.call-update) | async-done | bytes 5767184 | tf_op jit(solution)/shard_map/all_gather | solution.py:79
  431.9 7.5 %fusion.10 = f32[128,2048]{1,0:T(8,128)} fusion(bf16[1408,2048]{1,0:T(8,128)(2,1)} %all-gather.9.cloned.1.call-done, bf16[128,2048]{1,0:T(8,128)(2,1)S(1)} %copy-done.1, bf16[2048,1408]{1,0:T(8,128)(2,1)} %all-gather.7.cloned.1.call-done, f32[128,1408]{1,0:T(8,128)} %fusion.24), kind=kOutput, calls=%fused_computation.14 | convolution fusion | flops 1477476352 | bytes 13828096 | tf_op jit(solution)/shard_map/dot_general | solution.py:77
  439.4 0.1 copy.11
  439.5 6.4 %gather_fusion.1 = bf16[768,1024]{1,0:T(8,128)(2,1)} fusion(bf16[1024,1024]{1,0:T(8,128)(2,1)} %bitcast.7, s32[1024]{0:T(1024)S(1)} %pad_clamp_fusion), kind=kCustom, calls=%fused_computation.1 | custom fusion | bytes 3148800 | tf_op jit(solution)/shard_map/gather | solution.py:63
  445.9 3.9 reshape.78
  449.8 3.6 multiply_reduce_fusion
  453.4 1.8 add_convert_fusion
  (25 shorter events, 0.5 us)
Async XLA Ops:
  7.4 93.1 %copy-start = (bf16[1,704,2048]{2,1,0:T(8,128)(2,1)S(1)}, bf16[1,704,2048]{2,1,0:T(8,128)(2,1)}, u32[]{:S(2)}) copy-start(bf16[1,704,2048]{2,1,0:T(8,128)(2,1)} %param.17) | copy-start | bytes 8650756
  7.4 8.0 %copy-start.1 = (bf16[128,2048]{1,0:T(8,128)(2,1)S(1)}, bf16[128,2048]{1,0:T(8,128)(2,1)}, u32[]{:S(2)}) copy-start(bf16[128,2048]{1,0:T(8,128)(2,1)} %param.9) | copy-start | bytes 1572868
  7.4 85.3 %all-gather.11.cloned.1.call-start = ((), (), s32[]{:S(2)}) async-start(), calls=%async_computation.8 | async-start | bytes 6291456 | tf_op jit(solution)/shard_map/all_gather | solution.py:54
  80.5 44.5 %reduce-scatter.5.cloned.1.call-start = ((), (), s32[]{:S(2)}) async-start(), calls=%async_computation.9 | async-start | bytes 6291456 | tf_op jit(solution)/shard_map/reduce_scatter | solution.py:57
  111.8 120.5 %all-gather.5.cloned.1.call-start = ((), (), s32[]{:S(2)}) async-start(), calls=%async_computation.4 | async-start | bytes 6127616 | tf_op jit(solution)/shard_map/all_gather | solution.py:68
  112.4 210.0 %all-gather.7.cloned.1.call-start = ((), (), s32[]{:S(2)}) async-start(), calls=%async_computation.5 | async-start | bytes 6127616 | tf_op jit(solution)/shard_map/all_gather | solution.py:73
  113.0 318.9 %all-gather.9.cloned.1.call-start = ((), (), s32[]{:S(2)}) async-start(), calls=%async_computation.6 | async-start | bytes 6127616 | tf_op jit(solution)/shard_map/all_gather | solution.py:79
  125.0 314.5 %all-to-all-start.1 = ((bf16[16,64,1024]{2,1,0:T(8,128)(2,1)}), bf16[16,64,1024]{2,1,0:T(8,128)(2,1)}, u32[]{:S(2)}, u32[]{:S(2)}) async-start(bf16[16,64,1024]{2,1,0:T(8,128)(2,1)} %reduce-scatter.5.cloned.1.call-done), calls=%async_computation.3 | async-start | bytes 4194304 | tf_op jit(solution)/shard_map/all_to_all | solution.py:61
  132.0 321.4 %reduce-scatter.3.cloned.1.call-start = ((), (), s32[]{:S(2)}) async-start(), calls=%async_computation.7 | async-start | bytes 1572864 | tf_op jit(solution)/shard_map/reduce_scatter | solution.py:82
  236.8 202.5 %copy-start.2 = (f32[128,6]{0,1:T(8,128)S(1)}, f32[128,6]{0,1:T(8,128)}, u32[]{:S(2)}) copy-start(f32[128,6]{0,1:T(8,128)} %param.11) | copy-start | bytes 9220
Sparse Core Ops, SparseCore 0:
  80.6 11.9 all-gather.10
  111.9 13.0 reduce-scatter.4
  439.5 6.5 reduce-scatter.2
Sparse Core Ops, SparseCore 1:
  115.0 117.3 all-gather.4
  234.9 87.4 all-gather.6
  324.9 106.9 all-gather.8
where the time goes:
time: 463 us
  waiting for transfers between devices  320 us (69%)
  blocking collectives  57 us (12%)
  matrix products  31.1 us (7%)
  local copies, waits for them, and re-layouts  21.7 us (5%)
  between operations  14.9 us (3%)
  other arithmetic  10.1 us (2%)
  starting transfers between devices  7.34 us (2%)
    all_gather x1, waiting for transfers between devices, body(): lax.all_gather(shared_down, 'wide', axis=1, tiled=True)  110 us
    all_gather x1, waiting for transfers between devices, body(): lax.all_gather(shared_gate, 'wide', axis=0, tiled=True)  100 us
    all_gather x1, waiting for transfers between devices, body(): lax.all_gather(shared_up, 'wide', axis=0, tiled=True)  85.5 us
    all_to_all x1, blocking collectives, body(): lax.all_to_all(own_rows, 'wide', split_axis=0, concat_axis=0, tiled=True)  57 us
    all_gather x1, waiting for transfers between devices, body(): joined = lax.all_gather(arrived, 'narrow', axis=1, tiled=True)  12.1 us
    reduce_scatter x1, waiting for transfers between devices, body(): lax.psum_scatter(partial_value, 'narrow', scatter_dimension=2, tiled=True)  11.5 us
    dot_general x1, matrix products, expert_ffn(): jnp.dot(hidden, w_down, preferred_element_type=jnp.float32)  11.3 us
  transfers between devices with their start and end apart: 7, of which 5 were waited for; matrix products, arithmetic and copies ran while one was open for 6% of the time, Pallas kernels for 0%

commit v1 on v0

--- a/solution.py
+++ b/solution.py
@@ -76,7 +76,7 @@
     shared_hidden = (jax.nn.silu(gate_sum) * up_sum).astype(jnp.bfloat16)
     shared_terms = jnp.dot(
         shared_hidden,
-        lax.all_gather(shared_down, "wide", axis=1, tiled=True),
+        jnp.concatenate(lax.all_gather(shared_down, "wide"), axis=1),
         preferred_element_type=jnp.float32,
     )
     shared = lax.psum_scatter(shared_terms, "narrow", scatter_dimension=1, tiled=True)

time: 463 us -> 444 us (0.959)
  waiting for transfers between devices: 320 us -> 292 us
  local copies, waits for them, and re-layouts: 21.7 us -> 30 us
    all_gather x1, waiting for transfers between devices: 100 us -> 81.8 us  [body(): lax.all_gather(shared_gate, 'wide', axis=0, tiled=True)]
    all_gather x1, waiting for transfers between devices: 110 us -> 100 us  [body(): lax.all_gather(shared_down, 'wide')]
    reshape x0 -> x1, local copies, waits for them, and re-layouts: none -> 8.27 us  [body(): jnp.concatenate(lax.all_gather(shared_down, 'wide'), axis=1)]
  transfers between devices with their start and end apart: 7 -> 7, of which waited for: 5 -> 5; matrix products, arithmetic and copies ran while one was open for 6% -> 8% of each run, Pallas kernels for 0% -> 0%
where the time goes in v1:
time: 444 us
  waiting for transfers between devices  292 us (66%)
  blocking collectives  57 us (13%)
  matrix products  32.1 us (7%)
  local copies, waits for them, and re-layouts  30 us (7%)
  between operations  14.9 us (3%)
  other arithmetic  9.95 us (2%)
  starting transfers between devices  7.34 us (2%)
    all_gather x1, waiting for transfers between devices, body(): lax.all_gather(shared_down, 'wide')  100 us
    all_gather x1, waiting for transfers between devices, body(): lax.all_gather(shared_up, 'wide', axis=0, tiled=True)  85.3 us
    all_gather x1, waiting for transfers between devices, body(): lax.all_gather(shared_gate, 'wide', axis=0, tiled=True)  81.8 us
    all_to_all x1, blocking collectives, body(): lax.all_to_all(own_rows, 'wide', split_axis=0, concat_axis=0, tiled=True)  57 us
    all_gather x1, waiting for transfers between devices, body(): joined = lax.all_gather(arrived, 'narrow', axis=1, tiled=True)  12.1 us
    reduce_scatter x1, waiting for transfers between devices, body(): lax.psum_scatter(partial_value, 'narrow', scatter_dimension=2, tiled=True)  11.5 us
    dot_general x1, matrix products, expert_ffn(): jnp.dot(hidden, w_down, preferred_element_type=jnp.float32)  11.3 us
  transfers between devices with their start and end apart: 7, of which 5 were waited for; matrix products, arithmetic and copies ran while one was open for 8% of the time, Pallas kernels for 0%

profile of v1, /device:TPU:0, one launch (start us, length us, event | category | flops | bytes accessed | tf_op | source)
XLA Modules:
  0.0 443.7 jit_solution(6879990294401076113)
XLA Ops:
  7.4 0.9 copy.19
  8.3 0.1 eq.29
  8.5 0.1 eq.25
  8.6 0.7 broadcast_multiply_fusion
  9.3 1.7 reduce-window.6
  11.0 0.3 slice_reduce_fusion
  11.3 0.1 copy.18
  11.4 0.1 mul.50
  11.7 3.4 scatter_custom_fusion
  15.3 6.0 %gather_fusion = bf16[1024,2048]{1,0:T(8,128)(2,1)} fusion(bf16[128,2048]{1,0:T(8,128)(2,1)S(1)} %copy-done.1, s32[1024]{0:T(1024)S(1)} %fusion.17), kind=kCustom, calls=%fused_computation | custom fusion | bytes 8392704 | tf_op jit(solution)/shard_map/gather | solution.py:49
  21.3 2.0 dynamic-slice_select_fusion
  23.3 57.0 %all_to_all.10 = bf16[16,32,2048]{2,1,0:T(8,128)(2,1)} all-to-all(bf16[16,32,2048]{2,1,0:T(8,128)(2,1)S(1)} %dynamic-slice_select_fusion), channel_id=1, replica_groups=mesh['wide'=16,'narrow'=2] {'wide'}, dimensions={0} | all-to-all | bytes 4194304 | tf_op jit(solution)/shard_map/all_to_all | solution.py:53
  80.4 12.1 %all-gather.10.cloned.1.call-done = bf16[16,64,2048]{2,1,0:T(8,128)(2,1)} async-done(((bf16[16,32,2048]{2,1,0:T(8,128)(2,1)}), bf16[16,64,2048]{2,1,0:T(8,128)(2,1)}) %all-gather.10.cloned.1.call-update) | async-done | bytes 4194320 | tf_op jit(solution)/shard_map/all_gather | solution.py:54
  92.5 7.9 %fusion.1 = f32[1024,704]{0,1:T(8,128)} fusion(bf16[1024,2048]{1,0:T(8,128)(2,1)} %bitcast.53, bf16[1,2048,704]{1,2,0:T(8,128)(2,1)} %param.16), kind=kOutput, calls=%fused_computation.6 | convolution fusion | flops 2952790016 | bytes 9961472 | tf_op jit(solution)/shard_map/dot_general | solution.py:11
  100.4 11.3 %convolution_convert_fusion = bf16[1024,2048]{1,0:T(8,128)(2,1)} fusion(bf16[1,704,2048]{2,1,0:T(8,128)(2,1)S(1)} %copy-done, f32[1024,704]{0,1:T(8,128)} %fusion.1, bf16[1024,2048]{1,0:T(8,128)(2,1)} %bitcast.54, bf16[1,2048,704]{1,2,0:T(8,128)(2,1)} %param.15), kind=kOutput, calls=%fused_computation.4 | convolution fusion | flops 5912002560 | bytes 17039360 | tf_op jit(solution)/shard_map/dot_general | solution.py:13
  111.7 0.5 all-gather.12.cloned.1.call-update
  112.3 0.5 all-gather.6.cloned.1.call-update
  112.9 0.5 all-gather.8.cloned.1.call-update
  113.4 11.5 %reduce-scatter.5.cloned.1.call-done = bf16[16,64,1024]{2,1,0:T(8,128)(2,1)} async-done(((bf16[16,64,2048]{2,1,0:T(8,128)(2,1)}), bf16[16,64,1024]{2,1,0:T(8,128)(2,1)}) %reduce-scatter.5.cloned.1.call-update) | async-done | bytes 2097168 | tf_op jit(solution)/shard_map/reduce_scatter | solution.py:57
  124.9 7.0 %all-to-all-start.1 = ((bf16[16,64,1024]{2,1,0:T(8,128)(2,1)}), bf16[16,64,1024]{2,1,0:T(8,128)(2,1)}, u32[]{:S(2)}, u32[]{:S(2)}) async-start(bf16[16,64,1024]{2,1,0:T(8,128)(2,1)} %reduce-scatter.5.cloned.1.call-done), calls=%async_computation.3 | async-start | bytes 4194304 | tf_op jit(solution)/shard_map/all_to_all | solution.py:61
  131.9 0.2 reduce-scatter.3.cloned.1.call-start
  132.1 100.1 %all-gather.12.cloned.1.call-done = bf16[22528,128]{1,0:T(8,128)(2,1)} async-done(((bf16[1408,128]{1,0:T(8,128)(2,1)}), bf16[22528,128]{1,0:T(8,128)(2,1)}) %all-gather.12.cloned.1.call-update) | async-done | bytes 5767184 | tf_op jit(solution)/shard_map/all_gather | solution.py:79
  232.2 8.3 %copy.16 = bf16[1408,16,128]{0,2,1:T(8,128)(2,1)} copy(bf16[1408,16,128]{2,0,1:T(8,128)(2,1)} %bitcast.49) | data formatting | bytes 11534336 | tf_op jit(solution)/shard_map/reshape | solution.py:79
  240.5 81.8 %all-gather.6.cloned.1.call-done = bf16[2048,1408]{1,0:T(8,128)(2,1)} async-done(((bf16[128,1408]{1,0:T(8,128)(2,1)}), bf16[2048,1408]{1,0:T(8,128)(2,1)}) %all-gather.6.cloned.1.call-update) | async-done | bytes 5767184 | tf_op jit(solution)/shard_map/all_gather | solution.py:68
  322.2 4.5 %fusion.24 = f32[128,1408]{1,0:T(8,128)} fusion(bf16[128,2048]{1,0:T(8,128)(2,1)S(1)} %copy-done.1, bf16[2048,1408]{1,0:T(8,128)(2,1)} %all-gather.6.cloned.1.call-done), kind=kOutput, calls=%fused_computation.43 | convolution fusion | flops 738197504 | bytes 7012352 | tf_op jit(solution)/shard_map/dot_general | solution.py:66
  326.7 85.3 %all-gather.8.cloned.1.call-done = bf16[2048,1408]{1,0:T(8,128)(2,1)} async-done(((bf16[128,1408]{1,0:T(8,128)(2,1)}), bf16[2048,1408]{1,0:T(8,128)(2,1)}) %all-gather.8.cloned.1.call-update) | async-done | bytes 5767184 | tf_op jit(solution)/shard_map/all_gather | solution.py:73
  412.1 8.4 %fusion.10 = f32[128,2048]{1,0:T(8,128)} fusion(bf16[1408,2048]{0,1:T(8,128)(2,1)} %bitcast.50, bf16[128,2048]{1,0:T(8,128)(2,1)S(1)} %copy-done.1, bf16[2048,1408]{1,0:T(8,128)(2,1)} %all-gather.8.cloned.1.call-done, f32[128,1408]{1,0:T(8,128)} %fusion.24), kind=kOutput, calls=%fused_computation.14 | convolution fusion | flops 1477476352 | bytes 13828096 | tf_op jit(solution)/shard_map/dot_general | solution.py:77
  420.5 0.1 copy.17
  420.7 6.4 %gather_fusion.1 = bf16[768,1024]{1,0:T(8,128)(2,1)} fusion(bf16[1024,1024]{1,0:T(8,128)(2,1)} %bitcast.10, s32[1024]{0:T(1024)S(1)} %pad_clamp_fusion), kind=kCustom, calls=%fused_computation.1 | custom fusion | bytes 3148800 | tf_op jit(solution)/shard_map/gather | solution.py:63
  427.1 3.9 reshape.86
  431.0 3.6 multiply_reduce_fusion
  434.6 1.8 add_convert_fusion
  (26 shorter events, 0.6 us)
Async XLA Ops:
  7.4 93.0 %copy-start = (bf16[1,704,2048]{2,1,0:T(8,128)(2,1)S(1)}, bf16[1,704,2048]{2,1,0:T(8,128)(2,1)}, u32[]{:S(2)}) copy-start(bf16[1,704,2048]{2,1,0:T(8,128)(2,1)} %param.17) | copy-start | bytes 8650756
  7.4 7.9 %copy-start.1 = (bf16[128,2048]{1,0:T(8,128)(2,1)S(1)}, bf16[128,2048]{1,0:T(8,128)(2,1)}, u32[]{:S(2)}) copy-start(bf16[128,2048]{1,0:T(8,128)(2,1)} %param.9) | copy-start | bytes 1572868
  7.4 85.1 %all-gather.10.cloned.1.call-start = ((), (), s32[]{:S(2)}) async-start(), calls=%async_computation.7 | async-start | bytes 6291456 | tf_op jit(solution)/shard_map/all_gather | solution.py:54
  80.4 44.5 %reduce-scatter.5.cloned.1.call-start = ((), (), s32[]{:S(2)}) async-start(), calls=%async_computation.8 | async-start | bytes 6291456 | tf_op jit(solution)/shard_map/reduce_scatter | solution.py:57
  111.7 120.5 %all-gather.12.cloned.1.call-start = ((), (), s32[]{:S(2)}) async-start(), calls=%async_computation.9 | async-start | bytes 6127616 | tf_op jit(solution)/shard_map/all_gather | solution.py:79
  112.3 210.0 %all-gather.6.cloned.1.call-start = ((), (), s32[]{:S(2)}) async-start(), calls=%async_computation.4 | async-start | bytes 6127616 | tf_op jit(solution)/shard_map/all_gather | solution.py:68
  112.9 299.2 %all-gather.8.cloned.1.call-start = ((), (), s32[]{:S(2)}) async-start(), calls=%async_computation.5 | async-start | bytes 6127616 | tf_op jit(solution)/shard_map/all_gather | solution.py:73
  124.9 295.7 %all-to-all-start.1 = ((bf16[16,64,1024]{2,1,0:T(8,128)(2,1)}), bf16[16,64,1024]{2,1,0:T(8,128)(2,1)}, u32[]{:S(2)}, u32[]{:S(2)}) async-start(bf16[16,64,1024]{2,1,0:T(8,128)(2,1)} %reduce-scatter.5.cloned.1.call-done), calls=%async_computation.3 | async-start | bytes 4194304 | tf_op jit(solution)/shard_map/all_to_all | solution.py:61
  131.9 302.7 %reduce-scatter.3.cloned.1.call-start = ((), (), s32[]{:S(2)}) async-start(), calls=%async_computation.6 | async-start | bytes 1572864 | tf_op jit(solution)/shard_map/reduce_scatter | solution.py:82
  412.1 8.4 %copy-start.2 = (f32[128,6]{0,1:T(8,128)S(1)}, f32[128,6]{0,1:T(8,128)}, u32[]{:S(2)}) copy-start(f32[128,6]{0,1:T(8,128)} %param.11) | copy-start | bytes 9220
Sparse Core Ops, SparseCore 0:
  80.5 11.9 all-gather.9
  111.8 13.0 reduce-scatter.4
  420.6 7.1 reduce-scatter.2
Sparse Core Ops, SparseCore 1:
  114.9 117.3 all-gather.11
  234.8 87.4 all-gather.5
  324.8 87.2 all-gather.7
